TPU v7x, 256 devices: a whole 4x4x8 slice. The times are simulated.
256 devices in a mesh: seg: 32 (over y_hi, z, core), tp: 8 (over y_lo, x).
Axes of the slice: x: 4, y: 4 (y_hi: 2, y_lo: 2; y = y_hi * 2 + y_lo), z: 8, core: 2. Of those that a mesh axis runs over, the one named last changes fastest.
Arguments:
- tokens: bfloat16 [256, 4096], P('seg'), may hold values from -6 to 6
- w_query: bfloat16 [4096, 4096], P(None, 'tp'), may hold values from -0.09375 to 0.09375
- w_key: bfloat16 [4096, 1024], P(None, 'tp'), may hold values from -0.09375 to 0.09375
- w_value: bfloat16 [4096, 1024], P(None, 'tp'), may hold values from -0.09375 to 0.09375
- w_out: bfloat16 [4096, 4096], P('tp'), may hold values from -0.09375 to 0.09375
- gate_bias: float32 [32], P('tp'), may hold values from -3 to 3
- mem_store: float32 [512, 8, 128, 128], P('seg', 'tp'), may hold values from -6 to 6
- norm_store: float32 [512, 8, 128], P('seg', 'tp'), may hold values from 0.02 to 0.2
- k_cache: bfloat16 [256, 2048, 1024], P('seg', None, 'tp'), may hold values from -2500 to 2500
- v_cache: bfloat16 [256, 2048, 1024], P('seg', None, 'tp'), may hold values from -6 to 6
- home_owner: int32 [256], P('seg'), may hold values from 0 to 31, as said below
- home_slot: int32 [256], P('seg'), may hold values from 0 to 15
- cache_len: int32 [256], P('seg'), may hold values from 1 to 2048
- win_start: int32 [256], P('seg'), may hold values from 0 to 1023
Outputs:
- output: bfloat16 [256, 4096], P('seg', 'tp')
Inputs may be any that keep to these rules, and one draw needn't show every extreme that they name: Request b's memory is row 16 * home_owner[b] + home_slot[b] of mem_store and norm_store; no two requests share a row, so one owner holds at most 16 requests, and some owner holds exactly 16.
All inputs are finite; a program needn't handle non-finite values.
Results may differ from a plain program's by a relative error of at most 0.0065.
The roundings to bfloat16 on the way count: a program that leaves them out, or rounds other values in their place, can miss the bound.
Values may be sent and summed in bfloat16 or wider, within the bound.
A program may use at most 128 MiB of HBM per device.

v0:
```python
import jax
import jax.numpy as jnp
from jax import lax
from jax.sharding import PartitionSpec as P

H = 32
KVH = 8
DH = 128


def cut_along(x, dim, devices):
    before, after = (x.shape[:dim], x.shape[dim + 1 :])
    return jnp.moveaxis(x.reshape(*before, devices, -1, *after), dim, 0)


def summed_on_arrival(x, axis, dim):
    tiles = cut_along(x, dim, lax.axis_size(axis))
    arrived = lax.all_to_all(tiles, axis, split_axis=0, concat_axis=0, tiled=True)
    return arrived.sum(axis=0)


def elu_plus(values):
    return jnp.where(values > 0, values + 1.0, jnp.exp(jnp.minimum(values, 0.0)))


def body(
    tokens,
    w_query,
    w_key,
    w_value,
    w_out,
    gate_bias,
    mem_store,
    norm_store,
    k_cache,
    v_cache,
    home_owner,
    home_slot,
    cache_len,
    win_start,
):
    row_count = tokens.shape[0]
    window = k_cache.shape[1]
    kv_local = k_cache.shape[2] // DH
    group_size = H // KVH
    head_count = kv_local * group_size
    slot_count = mem_store.shape[0]
    query = jnp.dot(tokens, w_query, preferred_element_type=jnp.float32).astype(jnp.bfloat16)
    key_new = jnp.dot(tokens, w_key, preferred_element_type=jnp.float32).astype(jnp.bfloat16)
    value_new = jnp.dot(tokens, w_value, preferred_element_type=jnp.float32).astype(jnp.bfloat16)
    query_heads = query.reshape(row_count, kv_local, group_size, DH)
    owner_count = lax.axis_size("seg")
    owned = jnp.arange(owner_count, dtype=jnp.int32)[:, None] == home_owner[None, :]
    outgoing = jnp.where(owned[:, :, None], query[None, :, :], jnp.zeros((), jnp.bfloat16))
    slot_sent = jnp.where(owned, home_slot[None, :], -1)
    queries_in = lax.all_to_all(outgoing, "seg", split_axis=0, concat_axis=0, tiled=True)
    wanted = lax.all_to_all(slot_sent, "seg", split_axis=0, concat_axis=0, tiled=True)
    source_count = queries_in.shape[0]
    item_count = queries_in.shape[1]
    onehot = (wanted[:, :, None] == jnp.arange(slot_count, dtype=jnp.int32)[None, None, :]).astype(
        jnp.float32
    )
    present = jnp.sum(onehot, axis=-1)
    raised = elu_plus(queries_in.astype(jnp.float32)).reshape(
        source_count, item_count, kv_local, group_size, DH
    )
    every_numer = jnp.einsum(
        "snkgi,tkij->snkgtj", raised, mem_store, precision=lax.Precision.HIGHEST
    )
    every_denom = jnp.einsum(
        "snkgi,tki->snkgt", raised, norm_store, precision=lax.Precision.HIGHEST
    )
    part_numer = jnp.einsum(
        "snkgtj,snt->snkgj", every_numer, onehot, precision=lax.Precision.HIGHEST
    )
    part_denom = jnp.einsum("snkgt,snt->snkg", every_denom, onehot, precision=lax.Precision.HIGHEST)
    part_denom = part_denom + (1.0 - present)[:, :, None, None]
    part_read = (part_numer / part_denom[..., None]).astype(jnp.bfloat16)
    part_read = part_read.reshape(source_count, item_count, head_count * DH)
    back_read = lax.all_to_all(part_read, "seg", split_axis=0, concat_axis=0, tiled=True)
    memory_read = jnp.sum(back_read.astype(jnp.float32), axis=0).reshape(
        row_count, kv_local, group_size, DH
    )
    score_scale = DH ** (-0.5)
    cache_keys = k_cache.reshape(row_count, window, kv_local, DH)
    cache_values = v_cache.reshape(row_count, window, kv_local, DH)
    scores = (
        jnp.einsum("rkgi,rjki->rkgj", query_heads, cache_keys, preferred_element_type=jnp.float32)
        * score_scale
    )
    own_key = key_new.reshape(row_count, kv_local, DH)
    own_score = (
        jnp.einsum("rkgi,rki->rkg", query_heads, own_key, preferred_element_type=jnp.float32)
        * score_scale
    )
    position = jnp.arange(window, dtype=jnp.int32)
    live_mask = (position[None, :] >= win_start[:, None]) & (position[None, :] < cache_len[:, None])
    live_four = live_mask[:, None, None, :]
    top_score = jnp.maximum(jnp.max(jnp.where(live_four, scores, -jnp.inf), axis=-1), own_score)
    weights = jnp.where(live_four, jnp.exp(scores - top_score[..., None]), 0.0)
    own_weight = jnp.exp(own_score - top_score)
    softmax_total = jnp.sum(weights, axis=-1) + own_weight
    probs = (weights / softmax_total[..., None]).astype(jnp.bfloat16)
    own_prob = (own_weight / softmax_total).astype(jnp.bfloat16)
    local_read = jnp.einsum(
        "rkgj,rjki->rkgi", probs, cache_values, preferred_element_type=jnp.float32
    )
    own_value = value_new.reshape(row_count, kv_local, 1, DH).astype(jnp.float32)
    local_read = local_read + own_prob.astype(jnp.float32)[..., None] * own_value
    mix_gate = jax.nn.sigmoid(gate_bias).reshape(kv_local, group_size)[None, :, :, None]
    attended = (mix_gate * memory_read + (1.0 - mix_gate) * local_read).astype(jnp.bfloat16)
    attended = attended.reshape(row_count, head_count * DH)
    partial_value = jnp.dot(attended, w_out, preferred_element_type=jnp.float32)
    return summed_on_arrival(partial_value, "tp", 1).astype(jnp.bfloat16)


def solution(mesh):
    placed = (
        P("seg", None),
        P(None, "tp"),
        P(None, "tp"),
        P(None, "tp"),
        P("tp", None),
        P("tp"),
        P("seg", "tp", None, None),
        P("seg", "tp", None),
        P("seg", None, "tp"),
        P("seg", None, "tp"),
        P("seg"),
        P("seg"),
        P("seg"),
        P("seg"),
    )
    return jax.shard_map(
        body, mesh=mesh, in_specs=placed, out_specs=P("seg", "tp"), check_vma=False
    )
```

profile of v0, /device:TPU:8, one launch (start us, length us, event | category | flops | bytes accessed | tf_op | source)
XLA Modules:
  0.0 92.5 jit_solution(16339887369718122985)
XLA Ops:
  0.0 1.4 %compare_select_fusion = s32[32,1,8]{2,1,0:T(1,128)} fusion(s32[8]{0:T(128)} %param.25, s32[8]{0:T(128)} %param.24), kind=kLoop, calls=%fused_computation.43 | loop fusion | flops 512 | bytes 1088 | tf_op jit(solution)/shard_map/jit(_where)/select_n | solution.py:55
  1.5 10.6 %all-to-all-start.1 = ((s32[32,1,8]{2,1,0:T(1,128)}), s32[32,1,8]{2,1,0:T(1,128)S(1)}, u32[]{:S(2)}, u32[]{:S(2)}) async-start(s32[32,1,8]{2,1,0:T(1,128)} %compare_select_fusion), calls=%async_computation.1 | async-start | bytes 32768 | tf_op jit(solution)/shard_map/all_to_all | solution.py:57
  12.1 0.8 iota_compare_fusion.3
  12.9 3.3 %convolution_convert_fusion = bf16[8,512]{1,0:T(8,128)(2,1)S(1)} fusion(bf16[8,4096]{1,0:T(8,128)(2,1)} %param.14, bf16[4096,512]{1,0:T(8,128)(2,1)} %param.15), kind=kOutput, calls=%fused_computation.10 | convolution fusion | flops 33558528 | bytes 4268032 | tf_op jit(solution)/shard_map/dot_general | solution.py:48
  16.2 0.2 fusion.8
  16.5 0.1 fusion.23
  16.5 0.8 broadcast_select_fusion
  17.3 0.1 fusion.25
  17.5 1.3 %select_reduce_fusion = (f32[8,4]{1,0:T(8,128)S(1)}, f32[8,4,2048]{2,1,0:T(4,128)S(1)}) fusion(pred[8,2048]{1,0:T(8,128)(4,1)S(1)} %fusion.23, bf16[8,2048,128]{2,1,0:T(8,128)(2,1)S(1)} %copy-done.1, bf16[8,4,128]{2,0,1:T(8,128)(2,1)S(1)} %bitcast.61), kind=kOutput, calls=%fused_computation.28 | convolution fusion | flops 16973792 | bytes 4481152 | tf_op jit(solution)/shard_map/rkgi,rjki->rkgj/dot_general | solution.py:88
  18.8 3.2 %all-to-all-done.1 = s32[32,1,8]{2,1,0:T(1,128)S(1)} async-done(((s32[32,1,8]{2,1,0:T(1,128)}), s32[32,1,8]{2,1,0:T(1,128)S(1)}, u32[]{:S(2)}, u32[]{:S(2)}) %all-to-all-start.1) | async-done | bytes 1056 | tf_op jit(solution)/shard_map/all_to_all | solution.py:57
  22.0 6.8 %all-to-all-start = ((bf16[32,8,512]{2,1,0:T(8,128)(2,1)}), bf16[32,8,512]{2,1,0:T(8,128)(2,1)S(1)}, u32[]{:S(2)}, u32[]{:S(2)}) async-start(bf16[32,8,512]{2,1,0:T(8,128)(2,1)} %broadcast_select_fusion), calls=%async_computation | async-start | bytes 524288 | tf_op jit(solution)/shard_map/all_to_all | solution.py:56
  28.8 0.1 copy.21
  28.9 0.1 copy.40
  29.0 0.1 copy.22
  29.1 0.5 copy.28
  29.6 13.6 %all-to-all-done = bf16[32,8,512]{2,1,0:T(8,128)(2,1)S(1)} async-done(((bf16[32,8,512]{2,1,0:T(8,128)(2,1)}), bf16[32,8,512]{2,1,0:T(8,128)(2,1)S(1)}, u32[]{:S(2)}, u32[]{:S(2)}) %all-to-all-start) | async-done | bytes 262176 | tf_op jit(solution)/shard_map/all_to_all | solution.py:56
  43.3 0.1 fusion.11
  43.4 0.2 reshape.223
  43.6 1.1 %fusion.3 = f32[32,8,4]{2,1,0:T(8,128)S(1)} fusion(f32[32,8,4,128]{3,2,1,0:T(4,128)S(1)} %reshape.223, f32[16,128,1,1]{1,0,3,2:T(8,128)S(1)} %bitcast.65, f32[32,8,16]{2,1,0:T(8,128)S(1)} %copy.40), kind=kOutput, calls=%fused_computation.5 | convolution fusion | flops 25197568 | bytes 552960 | tf_op jit(solution)/shard_map/snkgi,tki->snkgt/dot_general | solution.py:70
  44.7 0.3 copy.36
  45.0 6.7 %fusion.9 = f32[32,8,4,16,128]{4,1,3,2,0:T(8,128)S(1)} fusion(f32[16,1,128,128]{3,2,1,0:T(8,128)S(1)} %copy-done, bf16[32,8,512]{2,1,0:T(8,128)(2,1)S(1)} %all-to-all-done), kind=kOutput, calls=%fused_computation.16 | convolution fusion | flops 3221880832 | bytes 9699328 | tf_op jit(solution)/shard_map/snkgi,tkij->snkgtj/dot_general | solution.py:67
  51.7 3.7 %fusion = f32[32,8,1,4,128]{4,2,3,1,0:T(1,128)S(1)} fusion(pred[32,8,16,1,1]{2,3,4,1,0:T(4,128)(4,1)S(1)} %copy.28, f32[32,8,4,16,128]{4,1,3,2,0:T(8,128)S(1)} %fusion.9), kind=kOutput, calls=%fused_computation | convolution fusion | flops 25165824 | bytes 8916992 | tf_op jit(solution)/shard_map/snkgtj,snt->snkgj/dot_general | solution.py:73
  55.3 0.9 fusion.15
  56.3 3.9 %all-to-all-start.2 = ((bf16[32,8,512]{2,1,0:T(8,128)(2,1)}), bf16[32,8,512]{2,1,0:T(8,128)(2,1)S(1)}, u32[]{:S(2)}, u32[]{:S(2)}) async-start(bf16[32,8,512]{2,1,0:T(8,128)(2,1)} %fusion.15), calls=%async_computation.2 | async-start | bytes 524288 | tf_op jit(solution)/shard_map/all_to_all | solution.py:80
  60.1 0.3 fusion.16
  60.4 6.5 %copy.39 = bf16[4096,512]{1,0:T(8,128)(2,1)} copy(bf16[4096,512]{0,1:T(8,128)(2,1)} %bitcast.59) | data formatting | bytes 8388608 | tf_op jit(solution)/shard_map/dot_general | solution.py:113
  67.0 0.2 fusion.7
  67.2 7.6 %all-to-all-done.2 = bf16[32,8,512]{2,1,0:T(8,128)(2,1)S(1)} async-done(((bf16[32,8,512]{2,1,0:T(8,128)(2,1)}), bf16[32,8,512]{2,1,0:T(8,128)(2,1)S(1)}, u32[]{:S(2)}, u32[]{:S(2)}) %all-to-all-start.2) | async-done | bytes 262176 | tf_op jit(solution)/shard_map/all_to_all | solution.py:80
  74.9 2.9 %fusion.6 = bf16[8,4,128]{2,1,0:T(4,128)(2,1)S(1)} fusion(bf16[8,2048,128]{2,1,0:T(8,128)(2,1)} %param.23, f32[8,4,2048]{2,1,0:T(4,128)S(1)} %get-tuple-element.12, f32[8,4]{1,0:T(8,128)S(1)} %get-tuple-element.8, f32[8,4]{1,0:T(8,128)S(1)} %multiply_maximum_fusion, pred[8,2048]{1,0:T(8,128)(4,1)S(1)} %fusion.23, f32[8,4,128]{2,1,0:T(4,128)S(1)} %reshape.227, ...), kind=kOutput, calls=%fused_computation.11 | convolution fusion | flops 17063936 | bytes 4501920 | tf_op jit(solution)/shard_map/rkgj,rjki->rkgi/dot_general | solution.py:105
  77.8 3.4 %convolution_bitcast_fusion.1 = f32[8,8,512]{2,1,0:T(8,128)S(1)} fusion(bf16[8,512,1]{1,0,2:T(8,128)(2,1)S(1)} %reshape.239, bf16[8,512,512]{2,1,0:T(8,128)(2,1)} %bitcast.58), kind=kOutput, calls=%fused_computation.6 | convolution fusion | flops 33554432 | bytes 4333568 | tf_op jit(solution)/shard_map/dot_general | solution.py:113
  81.2 10.7 %all_to_all.21 = f32[8,8,512]{2,1,0:T(8,128)S(1)} all-to-all(f32[8,8,512]{2,1,0:T(8,128)S(1)} %convolution_bitcast_fusion.1), channel_id=1, replica_groups=mesh['seg'=32,'tp'=8] {'tp'}, dimensions={0} | all-to-all | bytes 262144 | tf_op jit(solution)/shard_map/all_to_all | solution.py:18
  91.8 0.6 reduce_sum.39
  (28 shorter events, 0.2 us)
Async XLA Ops:
  0.0 45.0 %copy-start = (f32[16,1,128,128]{3,2,1,0:T(8,128)S(1)}, f32[16,1,128,128]{3,2,1,0:T(8,128)}, u32[]{:S(2)}) copy-start(f32[16,1,128,128]{3,2,1,0:T(8,128)} %param.20) | copy-start | bytes 3145732
  0.0 16.2 %copy-start.4 = (bf16[8,4096]{1,0:T(8,128)(2,1)S(1)}, bf16[8,4096]{1,0:T(8,128)(2,1)}, u32[]{:S(2)}) copy-start(bf16[8,4096]{1,0:T(8,128)(2,1)} %param.14) | copy-start | bytes 196612
  0.0 16.2 %copy-start.2 = (bf16[4096,128]{1,0:T(8,128)(2,1)S(1)}, bf16[4096,128]{1,0:T(8,128)(2,1)}, u32[]{:S(2)}) copy-start(bf16[4096,128]{1,0:T(8,128)(2,1)} %param.16) | copy-start | bytes 3145732
  0.0 16.4 %copy-start.6 = (s32[8]{0:T(128)S(1)}, s32[8]{0:T(128)}, u32[]{:S(2)}) copy-start(s32[8]{0:T(128)} %param.26) | copy-start | bytes 100
  0.0 16.4 %copy-start.7 = (s32[8]{0:T(128)S(1)}, s32[8]{0:T(128)}, u32[]{:S(2)}) copy-start(s32[8]{0:T(128)} %param.27) | copy-start | bytes 100
  1.5 20.5 %all-to-all-start.1 = ((s32[32,1,8]{2,1,0:T(1,128)}), s32[32,1,8]{2,1,0:T(1,128)S(1)}, u32[]{:S(2)}, u32[]{:S(2)}) async-start(s32[32,1,8]{2,1,0:T(1,128)} %compare_select_fusion), calls=%async_computation.1 | async-start | bytes 32768 | tf_op jit(solution)/shard_map/all_to_all | solution.py:57
  12.1 5.4 %copy-start.1 = (bf16[8,2048,128]{2,1,0:T(8,128)(2,1)S(1)}, bf16[8,2048,128]{2,1,0:T(8,128)(2,1)}, u32[]{:S(2)}) copy-start(bf16[8,2048,128]{2,1,0:T(8,128)(2,1)} %param.22) | copy-start | bytes 12582916
  12.9 5.9 %copy-start.8 = (f32[4]{0:T(128)S(1)}, f32[4]{0:T(128)}, u32[]{:S(2)}) copy-start(f32[4]{0:T(128)} %param.19) | copy-start | bytes 52
  16.2 27.4 %copy-start.5 = (f32[16,1,128]{2,1,0:T(1,128)S(1)}, f32[16,1,128]{2,1,0:T(1,128)}, u32[]{:S(2)}) copy-start(f32[16,1,128]{2,1,0:T(1,128)} %param.21) | copy-start | bytes 24580
  22.0 21.3 %all-to-all-start = ((bf16[32,8,512]{2,1,0:T(8,128)(2,1)}), bf16[32,8,512]{2,1,0:T(8,128)(2,1)S(1)}, u32[]{:S(2)}, u32[]{:S(2)}) async-start(bf16[32,8,512]{2,1,0:T(8,128)(2,1)} %broadcast_select_fusion), calls=%async_computation | async-start | bytes 524288 | tf_op jit(solution)/shard_map/all_to_all | solution.py:56
  56.3 18.5 %all-to-all-start.2 = ((bf16[32,8,512]{2,1,0:T(8,128)(2,1)}), bf16[32,8,512]{2,1,0:T(8,128)(2,1)S(1)}, u32[]{:S(2)}, u32[]{:S(2)}) async-start(bf16[32,8,512]{2,1,0:T(8,128)(2,1)} %fusion.15), calls=%async_computation.2 | async-start | bytes 524288 | tf_op jit(solution)/shard_map/all_to_all | solution.py:80
  60.4 6.6 %copy-start.3 = (bf16[4096,128]{1,0:T(8,128)(2,1)S(1)}, bf16[4096,128]{1,0:T(8,128)(2,1)}, u32[]{:S(2)}) copy-start(bf16[4096,128]{1,0:T(8,128)(2,1)} %param.17) | copy-start | bytes 3145732
where the time goes:
time: 93.4 us; the launch traced here: 92.5 us
  waiting for transfers between devices  24.4 us (26%)
  matrix products  22.9 us (25%)
  starting transfers between devices  21.2 us (23%)
  blocking collectives  10.7 us (11%)
  local copies, waits for them, and re-layouts  7.8 us (8%)
  other arithmetic  5.21 us (6%)
    all_to_all x1, waiting for transfers between devices, body(): lax.all_to_all(outgoing, 'seg', split_axis=0, concat_axis=0, tiled=True)  13.6 us
    all_to_all x1, blocking collectives, summed_on_arrival(): lax.all_to_all(tiles, axis, split_axis=0, concat_axis=0, tiled=True)  10.7 us
    all_to_all x1, starting transfers between devices, body(): lax.all_to_all(slot_sent, 'seg', split_axis=0, concat_axis=0, tiled=True)  10.6 us
    all_to_all x1, waiting for transfers between devices, body(): lax.all_to_all(part_read, 'seg', split_axis=0, concat_axis=0, tiled=True)  7.56 us
    all_to_all x1, starting transfers between devices, body(): lax.all_to_all(outgoing, 'seg', split_axis=0, concat_axis=0, tiled=True)  6.79 us
    dot_general x1, matrix products, body(): jnp.einsum('snkgi,tkij->snkgtj', raised, mem_store, precision=lax.Precisi...  6.69 us
    dot_general x1, local copies, waits for them, and re-layouts, body(): partial_value = jnp.dot(attended, w_out, preferred_element_type=jnp.float32)  6.54 us
    all_to_all x1, starting transfers between devices, body(): lax.all_to_all(part_read, 'seg', split_axis=0, concat_axis=0, tiled=True)  3.87 us
  transfers between devices with their start and end apart: 3, of which 3 were waited for; matrix products, arithmetic and copies ran while one was open for 16% of the time, Pallas kernels for 0%

commit v1 on v0

v1 whole, which is shorter than its diff:
```python
import functools

import jax
import jax.numpy as jnp
from jax import lax
from jax.experimental import pallas as pl
from jax.experimental.pallas import tpu as pltpu
from jax.sharding import PartitionSpec as P

DH = 128
GROUP = 4
ROWS = 8
SLOTS = 16
HALF = 2 * DH
TILE = 2 * ROWS

F32 = jnp.float32
BF16 = jnp.bfloat16


def seg_dims(count):
    return {32: (2, 8, 2), 8: (2, 2, 2)}[count]


def tp_dims(count):
    return {8: (2, 4), 2: (2, 1)}[count]


def seg_offsets(dims):
    ny, nz, nc = dims
    found = []
    for dy in range(ny):
        for dz in range(nz):
            for dc in range(nc):
                if (dy, dz, dc) != (0, 0, 0):
                    found.append((-(2 * dy + min(dz, nz - dz)), dc, dy, dz))
    found.sort()
    return [(dy, dz, dc) for _, dc, dy, dz in found]


def tp_offsets(dims):
    ny, nx = dims
    found = []
    for dy in range(ny):
        for dx in range(nx):
            if (dy, dx) != (0, 0):
                found.append((-(dy + min(dx, nx - dx)), dy, dx))
    found.sort()
    return [(dy, dx) for _, dy, dx in found]


def iota(shape, dim):
    return lax.broadcasted_iota(jnp.int32, shape, dim)


def dot(a, b, dims=((1,), (0,))):
    return lax.dot_general(a, b, (dims, ((), ())), preferred_element_type=F32)


def stack_heads(x, rows):
    return jnp.concatenate(
        [x[:rows, :DH], x[:rows, DH:], x[rows:, :DH], x[rows:, DH:]], axis=0
    )


def kernel(
    seg_count,
    tp_count,
    gate_ref,
    owner_ref,
    slot_ref,
    len_ref,
    start_ref,
    tok_h,
    wq_h,
    wk_h,
    wv_h,
    wo_h,
    mem_h,
    norm_h,
    kc_h,
    vc_h,
    out_ref,
    tok,
    wq,
    wkv,
    wo,
    mem,
    norm,
    kc,
    vc,
    mem_hi,
    mem_lo,
    qbuf,
    cbuf,
    sel,
    sel_t,
    rsend,
    rrecv,
    tsend,
    trecv,
    score,
    dsem,
    qs,
    qr,
    cs,
    cr,
    rs,
    rr,
    ts,
    tr,
):
    sdims, tdims = seg_dims(seg_count), tp_dims(tp_count)
    soffs, toffs = seg_offsets(sdims), tp_offsets(tdims)
    me = lax.axis_index("seg")
    my_t = lax.axis_index("tp")
    _, nz, nc = sdims
    my_y, my_z, my_c = me // (nz * nc), (me // nc) % nz, me % nc
    nx = tdims[1]
    my_ty, my_x = my_t // nx, my_t % nx

    def seg_to(off, sign):
        dy, dz, dc = off
        y = (my_y + dy) % sdims[0]
        z = (my_z + sign * dz + nz) % nz
        c = (my_c + dc) % nc
        return (y * nz + z) * nc + c

    def tp_to(off, sign):
        dy, dx = off
        return ((my_ty + dy) % tdims[0]) * nx + (my_x + sign * dx + nx) % nx

    chunks_q, kq = wq.shape[0], wq.shape[1]
    chunks_c, nj = kc.shape[0], kc.shape[2]
    loads = {}
    count = [0]

    def load(name, src, dst):
        loads[name] = pltpu.make_async_copy(src, dst, dsem.at[count[0]])
        count[0] += 1
        loads[name].start()

    load("tok", tok_h, tok)
    for k in range(chunks_q):
        load(f"wq{k}", wq_h.at[pl.ds(k * kq, kq), :], wq.at[k])

    def later():
        load("wk", wk_h, wkv.at[:, pl.ds(0, DH)])
        load("wv", wv_h, wkv.at[:, pl.ds(DH, DH)])
        yield
        load("mem", mem_h, mem)
        load("norm", norm_h, norm)
        yield
        for c in range(chunks_c):
            load(f"k{c}", kc_h.at[:, pl.ds(c * nj, nj), :], kc.at[c])
            yield
        for c in range(chunks_c):
            load(f"v{c}", vc_h.at[:, pl.ds(c * nj, nj), :], vc.at[c])
            yield
        ncol = wo.shape[2]
        for k, off in enumerate(toffs + [(0, 0)]):
            column = pl.multiple_of(tp_to(off, 1) * ncol, ncol)
            load(f"wo{k}", wo_h.at[:, pl.ds(column, ncol)], wo.at[k])
            yield

    pending = later()

    barrier = pltpu.get_barrier_semaphore()
    for off in soffs:
        pl.semaphore_signal(barrier, inc=1, device_id={"seg": seg_to(off, 1)})
    for off in toffs:
        pl.semaphore_signal(barrier, inc=1, device_id={"tp": tp_to(off, 1)})

    lane = iota((1, DH), 1)
    codes = jnp.zeros((1, DH), F32)
    for r in range(ROWS):
        code = (owner_ref[r] * SLOTS + slot_ref[r] - 256).astype(F32)
        codes = jnp.where(lane % ROWS == r, code, codes)
    cbuf[0] = codes

    loads["tok"].wait()
    acc = jnp.zeros((ROWS, GROUP * DH), F32)
    for k in range(chunks_q):
        loads[f"wq{k}"].wait()
        acc = acc + dot(tok[:, pl.ds(k * kq, kq)], wq[k])
        next(pending, None)
    query = acc.astype(BF16).astype(F32)
    qbuf[pl.ds(0, TILE), :] = jnp.concatenate(
        [query[:, :HALF], query[:, HALF:]], axis=0
    ).astype(BF16)
    for _ in pending:
        pass

    pl.semaphore_wait(barrier, len(soffs) + len(toffs))
    code_copies, query_copies = [], []
    for k, off in enumerate(soffs):
        target = {"seg": seg_to(off, 1)}
        copy = pltpu.make_async_remote_copy(
            cbuf.at[0], cbuf.at[k + 1], cs.at[k], cr.at[k], device_id=target
        )
        copy.start()
        code_copies.append(copy)
    for k, off in enumerate(soffs):
        target = {"seg": seg_to(off, 1)}
        copy = pltpu.make_async_remote_copy(
            qbuf.at[pl.ds(0, TILE)],
            qbuf.at[pl.ds((k + 1) * TILE, TILE)],
            qs.at[k],
            qr.at[k],
            device_id=target,
        )
        copy.start()
        query_copies.append(copy)

    loads["mem"].wait()
    loads["norm"].wait()
    flat = mem[...].reshape(SLOTS * DH, DH)
    high = flat.astype(BF16)
    mem_hi[...] = high
    mem_lo[...] = (flat - high.astype(F32)).astype(BF16)

    loads["wk"].wait()
    loads["wv"].wait()
    both = dot(tok[...], wkv[...]).astype(BF16).astype(F32)
    key_new, value_new = both[:, :DH], both[:, DH:]

    nr = GROUP * ROWS
    q32 = jnp.concatenate([query[:, h * DH : (h + 1) * DH] for h in range(GROUP)], axis=0)
    row32 = iota((nr, DH), 0) % ROWS
    scale = DH ** (-0.5)
    own = jnp.sum(q32 * jnp.concatenate([key_new] * GROUP, axis=0), axis=1, keepdims=True)
    own = own * scale

    row1 = iota((nr, 1), 0) % ROWS
    first = jnp.zeros((nr, 1), jnp.int32)
    last = jnp.zeros((nr, 1), jnp.int32)
    for r in range(ROWS):
        first = jnp.where(row1 == r, start_ref[r], first)
        last = jnp.where(row1 == r, len_ref[r], last)

    spread = jnp.concatenate(
        [jnp.where(row32 == r, q32, 0.0) for r in range(ROWS)], axis=1
    ).astype(BF16)
    top = own
    for c in range(chunks_c):
        loads[f"k{c}"].wait()
        keys = jnp.concatenate([kc[c, r] for r in range(ROWS)], axis=1)
        s = dot(spread, keys, ((1,), (1,))) * scale
        position = iota((nr, nj), 1) + c * nj
        s = jnp.where((position >= first) & (position < last), s, -jnp.inf)
        score[c] = s
        top = jnp.maximum(top, jnp.max(s, axis=1, keepdims=True))

    for copy in code_copies:
        copy.wait_recv()
    nmsg = seg_count * TILE
    arrived = cbuf[...].reshape(seg_count, DH).astype(BF16)
    which = (iota((nmsg, seg_count), 0) // TILE == iota((nmsg, seg_count), 1)).astype(F32)
    spread_codes = dot(which.astype(BF16), arrived)
    mrow, mlane = iota((nmsg, DH), 0) % TILE, iota((nmsg, DH), 1)
    code_col = jnp.sum(jnp.where(mrow == mlane, spread_codes, 0.0), axis=1, keepdims=True)
    wanted = (me * SLOTS - 256 + mlane % SLOTS).astype(F32)
    hit = (code_col == wanted) & (mlane // SLOTS == mrow // ROWS)
    picks = jnp.where(hit, 1.0, 0.0)
    sel_t[...] = picks.astype(BF16)
    sel[...] = picks.T[: 2 * SLOTS].astype(BF16)

    own_weight = jnp.exp(own - top)
    total = own_weight
    for c in range(chunks_c):
        w = jnp.exp(score[c] - top)
        score[c] = w
        total = total + jnp.sum(w, axis=1, keepdims=True)
    share = 1.0 / total
    own_prob = (own_weight * share).astype(BF16).astype(F32)

    for copy in query_copies:
        copy.wait_recv()
    lifted = stack_heads(dot(sel[...], qbuf[...]), SLOTS)
    lifted = jnp.where(lifted > 0, lifted + 1.0, jnp.exp(jnp.minimum(lifted, 0.0)))
    norms = jnp.concatenate([norm[...]] * GROUP, axis=0)
    denominator = jnp.sum(lifted * norms, axis=1, keepdims=True)
    nl = GROUP * SLOTS
    slot_row = iota((nl, DH), 0) % SLOTS
    part_hi = lifted.astype(BF16).astype(F32)
    part_lo = lifted - part_hi
    wide_hi = jnp.concatenate(
        [jnp.where(slot_row == t, part_hi, 0.0) for t in range(SLOTS)], axis=1
    ).astype(BF16)
    wide_lo = jnp.concatenate(
        [jnp.where(slot_row == t, part_lo, 0.0) for t in range(SLOTS)], axis=1
    ).astype(BF16)
    stacked = dot(jnp.concatenate([wide_hi, wide_lo], axis=0), mem_hi[...])
    numerator = stacked[:nl] + stacked[nl:] + dot(wide_hi, mem_lo[...])
    read = numerator / denominator
    parts = [read[h * SLOTS : (h + 1) * SLOTS] for h in range(GROUP)]
    read = jnp.concatenate(
        [
            jnp.concatenate(parts[:2], axis=1),
            jnp.concatenate(parts[2:], axis=1),
            jnp.zeros((DH - 2 * SLOTS, HALF), F32),
        ],
        axis=0,
    ).astype(BF16)
    rsend[...] = dot(sel_t[...], read).astype(BF16)
    read_copies = []
    for k, off in enumerate(soffs):
        copy = pltpu.make_async_remote_copy(
            rsend.at[pl.ds((k + 1) * TILE, TILE)],
            rrecv.at[pl.ds(k * TILE, TILE)],
            rs.at[k],
            rr.at[k],
            device_id={"seg": seg_to(off, -1)},
        )
        copy.start()
        read_copies.append(copy)

    wide = jnp.zeros((nr, ROWS * DH), F32)
    for c in range(chunks_c):
        loads[f"v{c}"].wait()
        values = jnp.concatenate([vc[c, r] for r in range(ROWS)], axis=1)
        wide = wide + dot((score[c] * share).astype(BF16), values)
    local = own_prob * jnp.concatenate([value_new] * GROUP, axis=0)
    for r in range(ROWS):
        local = local + jnp.where(row32 == r, wide[:, r * DH : (r + 1) * DH], 0.0)
    gates = jax.nn.sigmoid(
        jnp.concatenate([jnp.full((ROWS, DH), gate_ref[h], F32) for h in range(GROUP)], axis=0)
    )
    local = (1.0 - gates) * local
    for k in range(tp_count):
        loads[f"wo{k}"].wait()

    for copy in read_copies:
        copy.wait_recv()
    back = rsend[pl.ds(0, TILE), :].astype(F32)
    for k in range(len(soffs)):
        back = back + rrecv[pl.ds(k * TILE, TILE), :].astype(F32)
    mixed = gates * stack_heads(back, ROWS) + local
    attended = jnp.concatenate(
        [mixed[h * ROWS : (h + 1) * ROWS] for h in range(GROUP)], axis=1
    ).astype(BF16)

    out_copies = []
    for k, off in enumerate(toffs):
        tsend[k] = dot(attended, wo[k])
        copy = pltpu.make_async_remote_copy(
            tsend.at[k], trecv.at[k], ts.at[k], tr.at[k], device_id={"tp": tp_to(off, 1)}
        )
        copy.start()
        out_copies.append(copy)
    result = dot(attended, wo[tp_count - 1])
    for k, copy in enumerate(out_copies):
        copy.wait_recv()
    for k in range(len(toffs)):
        result = result + trecv[k]
    out_ref[...] = result.astype(BF16)
    for copy in code_copies + query_copies + read_copies + out_copies:
        copy.wait_send()


def body(
    tokens,
    w_query,
    w_key,
    w_value,
    w_out,
    gate_bias,
    mem_store,
    norm_store,
    k_cache,
    v_cache,
    home_owner,
    home_slot,
    cache_len,
    win_start,
):
    seg_count, tp_count = lax.axis_size("seg"), lax.axis_size("tp")
    depth = tokens.shape[1]
    window = k_cache.shape[1]
    width = w_query.shape[1]
    chunks_q, chunks_c = 8, 4
    nj = window // chunks_c
    columns = w_out.shape[1] // tp_count
    peers, partners = seg_count - 1, tp_count - 1
    nmsg = seg_count * TILE
    smem = pl.BlockSpec(memory_space=pltpu.SMEM)
    anywhere = pl.BlockSpec(memory_space=pl.ANY)
    dma = pltpu.SemaphoreType.DMA
    loads = 1 + chunks_q + 4 + 2 * chunks_c + tp_count
    return pl.pallas_call(
        functools.partial(kernel, seg_count, tp_count),
        out_shape=jax.ShapeDtypeStruct((ROWS, columns), BF16),
        in_specs=[smem] * 5 + [anywhere] * 9,
        out_specs=pl.BlockSpec(memory_space=pltpu.VMEM),
        scratch_shapes=[
            pltpu.VMEM((ROWS, depth), BF16),
            pltpu.VMEM((chunks_q, depth // chunks_q, width), BF16),
            pltpu.VMEM((depth, 2 * DH), BF16),
            pltpu.VMEM((tp_count, width, columns), BF16),
            pltpu.VMEM((SLOTS, DH, DH), F32),
            pltpu.VMEM((SLOTS, DH), F32),
            pltpu.VMEM((chunks_c, ROWS, nj, DH), BF16),
            pltpu.VMEM((chunks_c, ROWS, nj, DH), BF16),
            pltpu.VMEM((SLOTS * DH, DH), BF16),
            pltpu.VMEM((SLOTS * DH, DH), BF16),
            pltpu.VMEM((nmsg, HALF), BF16),
            pltpu.VMEM((seg_count, 1, DH), F32),
            pltpu.VMEM((2 * SLOTS, nmsg), BF16),
            pltpu.VMEM((nmsg, DH), BF16),
            pltpu.VMEM((nmsg, HALF), BF16),
            pltpu.VMEM((peers * TILE, HALF), BF16),
            pltpu.VMEM((partners, ROWS, columns), F32),
            pltpu.VMEM((partners, ROWS, columns), F32),
            pltpu.VMEM((chunks_c, GROUP * ROWS, nj), F32),
            dma((loads,)),
            dma((peers,)),
            dma((peers,)),
            dma((peers,)),
            dma((peers,)),
            dma((peers,)),
            dma((peers,)),
            dma((partners,)),
            dma((partners,)),
        ],
        compiler_params=pltpu.CompilerParams(
            collective_id=0, has_side_effects=True, vmem_limit_bytes=60 * 1024 * 1024
        ),
    )(
        gate_bias,
        home_owner,
        home_slot,
        cache_len,
        win_start,
        tokens,
        w_query,
        w_key,
        w_value,
        w_out,
        mem_store.reshape(SLOTS, DH, DH),
        norm_store.reshape(SLOTS, DH),
        k_cache,
        v_cache,
    )


def solution(mesh):
    placed = (
        P("seg", None),
        P(None, "tp"),
        P(None, "tp"),
        P(None, "tp"),
        P("tp", None),
        P("tp"),
        P("seg", "tp", None, None),
        P("seg", "tp", None),
        P("seg", None, "tp"),
        P("seg", None, "tp"),
        P("seg"),
        P("seg"),
        P("seg"),
        P("seg"),
    )
    return jax.shard_map(
        body, mesh=mesh, in_specs=placed, out_specs=P("seg", "tp"), check_vma=False
    )
```

time: 93.4 us -> 39.7 us (0.43)
  the two profiles are of different devices: /device:TPU:8 before, /device:TPU:1 now
where the time goes in v1:
time: 39.7 us; the launch traced here: 39.5 us
  Pallas kernels  38.2 us (96%)
  local copies, waits for them, and re-layouts  1.3 us (3%)
    pallas_call x1, Pallas kernels, body(): pl.pallas_call(functools.partial(kernel, seg_count, tp_count), out_shape=...  38.2 us
    unnamed x1, local copies, waits for them, and re-layouts  1.3 us

profile of v1, /device:TPU:1, one launch (start us, length us, event | category | flops | bytes accessed | tf_op | source)
XLA Modules:
  0.0 39.5 jit_solution(5974862792922294431)
XLA Ops:
  0.0 38.2 %shard_map.136 = bf16[8,512]{1,0:T(8,128)(2,1)} custom-call(f32[4]{0:T(128)} %gate_ref.1, s32[8]{0:T(128)} %owner_ref.1, s32[8]{0:T(128)} %slot_ref.1, s32[8]{0:T(128)} %len_ref.1, s32[8]{0:T(128)} %start_ref.1, bf16[8,4096]{1,0:T(8,128)(2,1)} %tok_h.1, bf16[4096,512]{1,0:T(8,128)(2,1)} %wq_h.1, bf16[4096,128]{1,0:T(8,128)(2,1)} %wk_h.1, ...), custom_call_target="tpu_custom_call" | custom-call | tf_op jit(solution)/shard_map/pallas_call | solution.py:390
  38.2 1.3 %copy.16 = bf16[8,512]{1,0:T(8,128)(2,1)} copy(bf16[8,512]{1,0:T(8,128)(2,1)} %shard_map.136) | data formatting | bytes 16384

commit v2 on v1

--- a/solution.py
+++ b/solution.py
@@ -27,15 +27,14 @@
 
 
 def seg_offsets(dims):
-    ny, nz, nc = dims
+    ny, nz, _ = dims
     found = []
     for dy in range(ny):
         for dz in range(nz):
-            for dc in range(nc):
-                if (dy, dz, dc) != (0, 0, 0):
-                    found.append((-(2 * dy + min(dz, nz - dz)), dc, dy, dz))
+            if (dy, dz) != (0, 0):
+                found.append((-(2 * dy + min(dz, nz - dz)), dy, dz))
     found.sort()
-    return [(dy, dz, dc) for _, dc, dy, dz in found]
+    return [(dy, dz, 0) for _, dy, dz in found]
 
 
 def tp_offsets(dims):
@@ -63,14 +62,19 @@
     )
 
 
+def stack_halves(x):
+    half = x.shape[1] // 2
+    return jnp.concatenate([x[:, :half], x[:, half:]], axis=0)
+
+
 def kernel(
     seg_count,
     tp_count,
-    gate_ref,
-    owner_ref,
-    slot_ref,
-    len_ref,
-    start_ref,
+    gate_h,
+    owner_h,
+    slot_h,
+    len_h,
+    start_h,
     tok_h,
     wq_h,
     wk_h,
@@ -81,6 +85,11 @@
     kc_h,
     vc_h,
     out_ref,
+    gate_ref,
+    owner_ref,
+    slot_ref,
+    len_ref,
+    start_ref,
     tok,
     wq,
     wkv,
@@ -95,6 +104,8 @@
     cbuf,
     sel,
     sel_t,
+    xbuf,
+    rbuf,
     rsend,
     rrecv,
     tsend,
@@ -109,6 +120,8 @@
     rr,
     ts,
     tr,
+    ps,
+    pr,
 ):
     sdims, tdims = seg_dims(seg_count), tp_dims(tp_count)
     soffs, toffs = seg_offsets(sdims), tp_offsets(tdims)
@@ -130,6 +143,13 @@
         dy, dx = off
         return ((my_ty + dy) % tdims[0]) * nx + (my_x + sign * dx + nx) % nx
 
+    barrier = pltpu.get_barrier_semaphore()
+    partner = (0, 0, 1)
+    for off in soffs + [partner]:
+        pl.semaphore_signal(barrier, inc=1, device_id={"seg": seg_to(off, 1)})
+    for off in toffs:
+        pl.semaphore_signal(barrier, inc=1, device_id={"tp": tp_to(off, 1)})
+
     chunks_q, kq = wq.shape[0], wq.shape[1]
     chunks_c, nj = kc.shape[0], kc.shape[2]
     loads = {}
@@ -141,6 +161,8 @@
         loads[name].start()
 
     load("tok", tok_h, tok)
+    load("owner", owner_h, owner_ref)
+    load("slot", slot_h, slot_ref)
     for k in range(chunks_q):
         load(f"wq{k}", wq_h.at[pl.ds(k * kq, kq), :], wq.at[k])
 
@@ -148,6 +170,9 @@
         load("wk", wk_h, wkv.at[:, pl.ds(0, DH)])
         load("wv", wv_h, wkv.at[:, pl.ds(DH, DH)])
         yield
+        load("gate", gate_h, gate_ref)
+        load("len", len_h, len_ref)
+        load("start", start_h, start_ref)
         load("mem", mem_h, mem)
         load("norm", norm_h, norm)
         yield
@@ -165,19 +190,6 @@
 
     pending = later()
 
-    barrier = pltpu.get_barrier_semaphore()
-    for off in soffs:
-        pl.semaphore_signal(barrier, inc=1, device_id={"seg": seg_to(off, 1)})
-    for off in toffs:
-        pl.semaphore_signal(barrier, inc=1, device_id={"tp": tp_to(off, 1)})
-
-    lane = iota((1, DH), 1)
-    codes = jnp.zeros((1, DH), F32)
-    for r in range(ROWS):
-        code = (owner_ref[r] * SLOTS + slot_ref[r] - 256).astype(F32)
-        codes = jnp.where(lane % ROWS == r, code, codes)
-    cbuf[0] = codes
-
     loads["tok"].wait()
     acc = jnp.zeros((ROWS, GROUP * DH), F32)
     for k in range(chunks_q):
@@ -185,13 +197,20 @@
         acc = acc + dot(tok[:, pl.ds(k * kq, kq)], wq[k])
         next(pending, None)
     query = acc.astype(BF16).astype(F32)
-    qbuf[pl.ds(0, TILE), :] = jnp.concatenate(
-        [query[:, :HALF], query[:, HALF:]], axis=0
-    ).astype(BF16)
+    qbuf[pl.ds(0, TILE), :] = stack_halves(query).astype(BF16)
     for _ in pending:
         pass
 
-    pl.semaphore_wait(barrier, len(soffs) + len(toffs))
+    loads["owner"].wait()
+    loads["slot"].wait()
+    lane = iota((1, DH), 1)
+    codes = jnp.zeros((1, DH), F32)
+    for r in range(ROWS):
+        code = (owner_ref[r] * SLOTS + slot_ref[r] - 256).astype(F32)
+        codes = jnp.where(lane % ROWS == r, code, codes)
+    cbuf[0] = codes
+
+    pl.semaphore_wait(barrier, len(soffs) + 1 + len(toffs))
     code_copies, query_copies = [], []
     for k, off in enumerate(soffs):
         target = {"seg": seg_to(off, 1)}
@@ -231,6 +250,8 @@
     own = jnp.sum(q32 * jnp.concatenate([key_new] * GROUP, axis=0), axis=1, keepdims=True)
     own = own * scale
 
+    for name in ("gate", "len", "start"):
+        loads[name].wait()
     row1 = iota((nr, 1), 0) % ROWS
     first = jnp.zeros((nr, 1), jnp.int32)
     last = jnp.zeros((nr, 1), jnp.int32)
@@ -238,6 +259,7 @@
         first = jnp.where(row1 == r, start_ref[r], first)
         last = jnp.where(row1 == r, len_ref[r], last)
 
+    rbuf[pl.ds(4 * SLOTS, DH - 4 * SLOTS), :] = jnp.zeros((DH - 4 * SLOTS, HALF), BF16)
     spread = jnp.concatenate(
         [jnp.where(row32 == r, q32, 0.0) for r in range(ROWS)], axis=1
     ).astype(BF16)
@@ -253,17 +275,19 @@
 
     for copy in code_copies:
         copy.wait_recv()
-    nmsg = seg_count * TILE
-    arrived = cbuf[...].reshape(seg_count, DH).astype(BF16)
-    which = (iota((nmsg, seg_count), 0) // TILE == iota((nmsg, seg_count), 1)).astype(F32)
+    senders = cbuf.shape[0]
+    nmsg = senders * TILE
+    arrived = cbuf[...].reshape(senders, DH).astype(BF16)
+    which = (iota((nmsg, senders), 0) // TILE == iota((nmsg, senders), 1)).astype(F32)
     spread_codes = dot(which.astype(BF16), arrived)
     mrow, mlane = iota((nmsg, DH), 0) % TILE, iota((nmsg, DH), 1)
     code_col = jnp.sum(jnp.where(mrow == mlane, spread_codes, 0.0), axis=1, keepdims=True)
-    wanted = (me * SLOTS - 256 + mlane % SLOTS).astype(F32)
-    hit = (code_col == wanted) & (mlane // SLOTS == mrow // ROWS)
+    holder = jnp.where(mlane < 2 * SLOTS, me, seg_to(partner, 1))
+    wanted = (holder * SLOTS - 256 + mlane % SLOTS).astype(F32)
+    hit = (code_col == wanted) & ((mlane // SLOTS) % 2 == mrow // ROWS) & (mlane < 4 * SLOTS)
     picks = jnp.where(hit, 1.0, 0.0)
     sel_t[...] = picks.astype(BF16)
-    sel[...] = picks.T[: 2 * SLOTS].astype(BF16)
+    sel[...] = picks.T[: 4 * SLOTS].astype(BF16)
 
     own_weight = jnp.exp(own - top)
     total = own_weight
@@ -276,7 +300,17 @@
 
     for copy in query_copies:
         copy.wait_recv()
-    lifted = stack_heads(dot(sel[...], qbuf[...]), SLOTS)
+    picked = dot(sel[...], qbuf[...])
+    own_half, other_half = pl.ds(0, 2 * SLOTS), pl.ds(2 * SLOTS, 2 * SLOTS)
+    xbuf[own_half, :] = picked[2 * SLOTS :].astype(BF16)
+    other = {"seg": seg_to(partner, 1)}
+    pick_copy = pltpu.make_async_remote_copy(
+        xbuf.at[own_half], xbuf.at[other_half], ps.at[0], pr.at[0], device_id=other
+    )
+    pick_copy.start()
+    pick_copy.wait_recv()
+    picked = picked[: 2 * SLOTS] + xbuf[other_half, :].astype(F32)
+    lifted = stack_heads(picked, SLOTS)
     lifted = jnp.where(lifted > 0, lifted + 1.0, jnp.exp(jnp.minimum(lifted, 0.0)))
     norms = jnp.concatenate([norm[...]] * GROUP, axis=0)
     denominator = jnp.sum(lifted * norms, axis=1, keepdims=True)
@@ -294,15 +328,15 @@
     numerator = stacked[:nl] + stacked[nl:] + dot(wide_hi, mem_lo[...])
     read = numerator / denominator
     parts = [read[h * SLOTS : (h + 1) * SLOTS] for h in range(GROUP)]
-    read = jnp.concatenate(
-        [
-            jnp.concatenate(parts[:2], axis=1),
-            jnp.concatenate(parts[2:], axis=1),
-            jnp.zeros((DH - 2 * SLOTS, HALF), F32),
-        ],
-        axis=0,
+    rbuf[own_half, :] = jnp.concatenate(
+        [jnp.concatenate(parts[:2], axis=1), jnp.concatenate(parts[2:], axis=1)], axis=0
     ).astype(BF16)
-    rsend[...] = dot(sel_t[...], read).astype(BF16)
+    swap_copy = pltpu.make_async_remote_copy(
+        rbuf.at[own_half], rbuf.at[other_half], ps.at[1], pr.at[1], device_id=other
+    )
+    swap_copy.start()
+    swap_copy.wait_recv()
+    rsend[...] = dot(sel_t[...], rbuf[...]).astype(BF16)
     read_copies = []
     for k, off in enumerate(soffs):
         copy = pltpu.make_async_remote_copy(
@@ -342,19 +376,19 @@
 
     out_copies = []
     for k, off in enumerate(toffs):
-        tsend[k] = dot(attended, wo[k])
+        tsend[k] = stack_halves(dot(attended, wo[k])).astype(BF16)
         copy = pltpu.make_async_remote_copy(
             tsend.at[k], trecv.at[k], ts.at[k], tr.at[k], device_id={"tp": tp_to(off, 1)}
         )
         copy.start()
         out_copies.append(copy)
-    result = dot(attended, wo[tp_count - 1])
+    result = stack_halves(dot(attended, wo[tp_count - 1]))
     for k, copy in enumerate(out_copies):
         copy.wait_recv()
     for k in range(len(toffs)):
-        result = result + trecv[k]
-    out_ref[...] = result.astype(BF16)
-    for copy in code_copies + query_copies + read_copies + out_copies:
+        result = result + trecv[k].astype(F32)
+    out_ref[...] = jnp.concatenate([result[:ROWS], result[ROWS:]], axis=1).astype(BF16)
+    for copy in code_copies + query_copies + read_copies + out_copies + [pick_copy, swap_copy]:
         copy.wait_send()
 
 
@@ -381,18 +415,23 @@
     chunks_q, chunks_c = 8, 4
     nj = window // chunks_c
     columns = w_out.shape[1] // tp_count
-    peers, partners = seg_count - 1, tp_count - 1
-    nmsg = seg_count * TILE
-    smem = pl.BlockSpec(memory_space=pltpu.SMEM)
+    senders = seg_count // seg_dims(seg_count)[2]
+    peers, partners = senders - 1, tp_count - 1
+    nmsg = senders * TILE
     anywhere = pl.BlockSpec(memory_space=pl.ANY)
     dma = pltpu.SemaphoreType.DMA
-    loads = 1 + chunks_q + 4 + 2 * chunks_c + tp_count
+    loads = 1 + chunks_q + 9 + 2 * chunks_c + tp_count
     return pl.pallas_call(
         functools.partial(kernel, seg_count, tp_count),
         out_shape=jax.ShapeDtypeStruct((ROWS, columns), BF16),
-        in_specs=[smem] * 5 + [anywhere] * 9,
+        in_specs=[anywhere] * 14,
         out_specs=pl.BlockSpec(memory_space=pltpu.VMEM),
         scratch_shapes=[
+            pltpu.SMEM((GROUP,), F32),
+            pltpu.SMEM((ROWS,), jnp.int32),
+            pltpu.SMEM((ROWS,), jnp.int32),
+            pltpu.SMEM((ROWS,), jnp.int32),
+            pltpu.SMEM((ROWS,), jnp.int32),
             pltpu.VMEM((ROWS, depth), BF16),
             pltpu.VMEM((chunks_q, depth // chunks_q, width), BF16),
             pltpu.VMEM((depth, 2 * DH), BF16),
@@ -404,13 +443,15 @@
             pltpu.VMEM((SLOTS * DH, DH), BF16),
             pltpu.VMEM((SLOTS * DH, DH), BF16),
             pltpu.VMEM((nmsg, HALF), BF16),
-            pltpu.VMEM((seg_count, 1, DH), F32),
-            pltpu.VMEM((2 * SLOTS, nmsg), BF16),
+            pltpu.VMEM((senders, 1, DH), F32),
+            pltpu.VMEM((4 * SLOTS, nmsg), BF16),
             pltpu.VMEM((nmsg, DH), BF16),
+            pltpu.VMEM((4 * SLOTS, HALF), BF16),
+            pltpu.VMEM((DH, HALF), BF16),
             pltpu.VMEM((nmsg, HALF), BF16),
             pltpu.VMEM((peers * TILE, HALF), BF16),
-            pltpu.VMEM((partners, ROWS, columns), F32),
-            pltpu.VMEM((partners, ROWS, columns), F32),
+            pltpu.VMEM((partners, 2 * ROWS, columns // 2), BF16),
+            pltpu.VMEM((partners, 2 * ROWS, columns // 2), BF16),
             pltpu.VMEM((chunks_c, GROUP * ROWS, nj), F32),
             dma((loads,)),
             dma((peers,)),
@@ -421,6 +462,8 @@
             dma((peers,)),
             dma((partners,)),
             dma((partners,)),
+            dma((2,)),
+            dma((2,)),
         ],
         compiler_params=pltpu.CompilerParams(
             collective_id=0, has_side_effects=True, vmem_limit_bytes=60 * 1024 * 1024

time: 39.7 us -> 33 us (0.83)
  the two profiles are of different devices: /device:TPU:1 before, /device:TPU:8 now
where the time goes in v2:
time: 33 us; the launch traced here: 32.8 us
  Pallas kernels  31.5 us (95%)
  local copies, waits for them, and re-layouts  1.3 us (4%)
    pallas_call x1, Pallas kernels, body(): pl.pallas_call(functools.partial(kernel, seg_count, tp_count), out_shape=...  31.5 us
    unnamed x1, local copies, waits for them, and re-layouts  1.3 us

profile of v2, /device:TPU:8, one launch (start us, length us, event | category | flops | bytes accessed | tf_op | source)
XLA Modules:
  0.0 32.8 jit_solution(602880788264519248)
XLA Ops:
  0.0 31.5 %shard_map.136 = bf16[8,512]{1,0:T(8,128)(2,1)} custom-call(f32[4]{0:T(128)} %gate_h.1, s32[8]{0:T(128)} %owner_h.1, s32[8]{0:T(128)} %slot_h.1, s32[8]{0:T(128)} %len_h.1, s32[8]{0:T(128)} %start_h.1, bf16[8,4096]{1,0:T(8,128)(2,1)} %tok_h.1, bf16[4096,512]{1,0:T(8,128)(2,1)} %wq_h.1, bf16[4096,128]{1,0:T(8,128)(2,1)} %wk_h.1, bf16[4096,128]{1,0:T(8,128)(2,1)} %wv_h.1, ...), custom_call_target="tpu_custom_call" | custom-call | tf_op jit(solution)/shard_map/pallas_call | solution.py:424
  31.5 1.3 %copy.16 = bf16[8,512]{1,0:T(8,128)(2,1)} copy(bf16[8,512]{1,0:T(8,128)(2,1)} %shard_map.136) | data formatting | bytes 16384

commit v3 on v2

--- a/solution.py
+++ b/solution.py
@@ -423,7 +423,7 @@
     loads = 1 + chunks_q + 9 + 2 * chunks_c + tp_count
     return pl.pallas_call(
         functools.partial(kernel, seg_count, tp_count),
-        out_shape=jax.ShapeDtypeStruct((ROWS, columns), BF16),
+        out_shape=pltpu.VMEM((ROWS, columns), BF16),
         in_specs=[anywhere] * 14,
         out_specs=pl.BlockSpec(memory_space=pltpu.VMEM),
         scratch_shapes=[

time: 33 us -> 31.6 us (0.958)
  local copies, waits for them, and re-layouts: 1.3 us -> 0.6 us
  Pallas kernels: 31.5 us -> 30.9 us
    unnamed x1, local copies, waits for them, and re-layouts: 1.3 us -> 0.6 us
    pallas_call x1, Pallas kernels: 31.5 us -> 30.9 us  [body(): pl.pallas_call(functools.partial(kernel, seg_count, tp_count), out_shape=...]
where the time goes in v3:
time: 31.6 us; the launch traced here: 31.5 us
  Pallas kernels  30.9 us (98%)
  local copies, waits for them, and re-layouts  0.6 us (2%)
    pallas_call x1, Pallas kernels, body(): pl.pallas_call(functools.partial(kernel, seg_count, tp_count), out_shape=...  30.9 us

profile of v3, /device:TPU:8, one launch (start us, length us, event | category | flops | bytes accessed | tf_op | source)
XLA Modules:
  0.0 31.5 jit_solution(56521595348177528)
XLA Ops:
  0.0 30.9 %shard_map.136 = bf16[8,512]{1,0:T(8,128)(2,1)S(1)} custom-call(f32[4]{0:T(128)} %gate_h.1, s32[8]{0:T(128)} %owner_h.1, s32[8]{0:T(128)} %slot_h.1, s32[8]{0:T(128)} %len_h.1, s32[8]{0:T(128)} %start_h.1, bf16[8,4096]{1,0:T(8,128)(2,1)} %tok_h.1, bf16[4096,512]{1,0:T(8,128)(2,1)} %wq_h.1, bf16[4096,128]{1,0:T(8,128)(2,1)} %wk_h.1, bf16[4096,128]{1,0:T(8,128)(2,1)} %wv_h.1, ...), custom_call_target="tpu_custom_call" | custom-call | tf_op jit(solution)/shard_map/pallas_call | solution.py:424
  30.9 0.6 %copy.16 = bf16[8,512]{1,0:T(8,128)(2,1)} copy(bf16[8,512]{1,0:T(8,128)(2,1)S(1)} %shard_map.136) | data formatting | bytes 16384

commit v4 on v3

--- a/solution.py
+++ b/solution.py
@@ -219,8 +219,6 @@
         )
         copy.start()
         code_copies.append(copy)
-    for k, off in enumerate(soffs):
-        target = {"seg": seg_to(off, 1)}
         copy = pltpu.make_async_remote_copy(
             qbuf.at[pl.ds(0, TILE)],
             qbuf.at[pl.ds((k + 1) * TILE, TILE)],

time: 31.6 us -> 31.5 us (level)
  no operation moved by 1% of the time
where the time goes in v4:
time: 31.5 us; the launch traced here: 31.4 us
  Pallas kernels  30.8 us (98%)
  local copies, waits for them, and re-layouts  0.6 us (2%)
    pallas_call x1, Pallas kernels, body(): pl.pallas_call(functools.partial(kernel, seg_count, tp_count), out_shape=...  30.8 us

profile of v4, /device:TPU:8, one launch (start us, length us, event | category | flops | bytes accessed | tf_op | source)
XLA Modules:
  0.0 31.4 jit_solution(16842044589251483345)
XLA Ops:
  0.0 30.8 %shard_map.136 = bf16[8,512]{1,0:T(8,128)(2,1)S(1)} custom-call(f32[4]{0:T(128)} %gate_h.1, s32[8]{0:T(128)} %owner_h.1, s32[8]{0:T(128)} %slot_h.1, s32[8]{0:T(128)} %len_h.1, s32[8]{0:T(128)} %start_h.1, bf16[8,4096]{1,0:T(8,128)(2,1)} %tok_h.1, bf16[4096,512]{1,0:T(8,128)(2,1)} %wq_h.1, bf16[4096,128]{1,0:T(8,128)(2,1)} %wk_h.1, bf16[4096,128]{1,0:T(8,128)(2,1)} %wv_h.1, ...), custom_call_target="tpu_custom_call" | custom-call | tf_op jit(solution)/shard_map/pallas_call | solution.py:422
  30.8 0.6 %copy.16 = bf16[8,512]{1,0:T(8,128)(2,1)} copy(bf16[8,512]{1,0:T(8,128)(2,1)S(1)} %shard_map.136) | data formatting | bytes 16384

commit v5 on v4

--- a/solution.py
+++ b/solution.py
@@ -32,7 +32,7 @@
     for dy in range(ny):
         for dz in range(nz):
             if (dy, dz) != (0, 0):
-                found.append((-(2 * dy + min(dz, nz - dz)), dy, dz))
+                found.append((-(6 * dy + min(dz, nz - dz)), dy, dz))
     found.sort()
     return [(dy, dz, 0) for _, dy, dz in found]
 
@@ -334,18 +334,23 @@
     )
     swap_copy.start()
     swap_copy.wait_recv()
-    rsend[...] = dot(sel_t[...], rbuf[...]).astype(BF16)
+    half_rows = rsend.shape[0] // 2
     read_copies = []
-    for k, off in enumerate(soffs):
-        copy = pltpu.make_async_remote_copy(
-            rsend.at[pl.ds((k + 1) * TILE, TILE)],
-            rrecv.at[pl.ds(k * TILE, TILE)],
-            rs.at[k],
-            rr.at[k],
-            device_id={"seg": seg_to(off, -1)},
-        )
-        copy.start()
-        read_copies.append(copy)
+    for part in range(2):
+        block = pl.ds(part * half_rows, half_rows)
+        rsend[block, :] = dot(sel_t[block, :], rbuf[...]).astype(BF16)
+        per_half = half_rows // TILE
+        for tile in range(max(1, part * per_half), (part + 1) * per_half):
+            k = tile - 1
+            copy = pltpu.make_async_remote_copy(
+                rsend.at[pl.ds(tile * TILE, TILE)],
+                rrecv.at[pl.ds(k * TILE, TILE)],
+                rs.at[k],
+                rr.at[k],
+                device_id={"seg": seg_to(soffs[k], -1)},
+            )
+            copy.start()
+            read_copies.append(copy)
 
     wide = jnp.zeros((nr, ROWS * DH), F32)
     for c in range(chunks_c):

time: 31.5 us -> 31.4 us (level)
  no operation moved by 1% of the time
where the time goes in v5:
time: 31.4 us; the launch traced here: 31.3 us
  Pallas kernels  30.7 us (98%)
  local copies, waits for them, and re-layouts  0.6 us (2%)
    pallas_call x1, Pallas kernels, body(): pl.pallas_call(functools.partial(kernel, seg_count, tp_count), out_shape=...  30.7 us

profile of v5, /device:TPU:8, one launch (start us, length us, event | category | flops | bytes accessed | tf_op | source)
XLA Modules:
  0.0 31.3 jit_solution(3029019089031699726)
XLA Ops:
  0.0 30.7 %shard_map.136 = bf16[8,512]{1,0:T(8,128)(2,1)S(1)} custom-call(f32[4]{0:T(128)} %gate_h.1, s32[8]{0:T(128)} %owner_h.1, s32[8]{0:T(128)} %slot_h.1, s32[8]{0:T(128)} %len_h.1, s32[8]{0:T(128)} %start_h.1, bf16[8,4096]{1,0:T(8,128)(2,1)} %tok_h.1, bf16[4096,512]{1,0:T(8,128)(2,1)} %wq_h.1, bf16[4096,128]{1,0:T(8,128)(2,1)} %wk_h.1, bf16[4096,128]{1,0:T(8,128)(2,1)} %wv_h.1, ...), custom_call_target="tpu_custom_call" | custom-call | tf_op jit(solution)/shard_map/pallas_call | solution.py:427
  30.7 0.6 %copy.16 = bf16[8,512]{1,0:T(8,128)(2,1)} copy(bf16[8,512]{1,0:T(8,128)(2,1)S(1)} %shard_map.136) | data formatting | bytes 16384
